TPU v7x, 32 devices: a whole 2x2x4 slice. The times are simulated.
32 devices in a mesh: seq: 8 (over z, x), mp: 4 (over y, core).
Axes of the slice: x: 2, y: 2, z: 4, core: 2. Of those that a mesh axis runs over, the one named last changes fastest.
Arguments:
- branch_in: bfloat16 [4096, 4096], P('seq', 'mp'), may hold values from -48 to 48
- branch_gate: bfloat16 [4096, 4096], P('seq', 'mp'), may hold values from -6 to 6
- conv_taps: float32 [4, 4096], P(None, 'mp'), may hold values from -3 to 3
- conv_shift: float32 [4096], P('mp'), may hold values from -3 to 3
- inflow_weight: bfloat16 [16, 256, 256], P('mp'), may hold values from -0.375 to 0.375
- inflow_bias: float32 [4096], P('mp'), may hold values from -4 to 4
- decay_weight: bfloat16 [16, 256, 256], P('mp'), may hold values from -0.375 to 0.375
- decay_bias: float32 [4096], P('mp'), may hold values from -12 to -1.5
- decay_param: float32 [4096], P('mp'), may hold values from 3 to 4
- stream: bfloat16 [4096, 4096], P('seq', 'mp'), may hold values from -48 to 48
- norm_gain: float32 [4096], P('mp'), may hold values from 0.5 to 1.5
- memory_weight: bfloat16 [4096, 512], P('mp'), may hold values from -1 to 1
- queries: bfloat16 [4096, 4096], P('seq', 'mp'), may hold values from -128 to 128
Outputs:
- recurrent_out: bfloat16 [4096, 4096], P('seq', 'mp')
- attended: bfloat16 [4096, 4096], P('seq', 'mp')
All inputs are finite; a program needn't handle non-finite values.
Results may differ from a plain program's by a relative error of at most 0.0071.
Values may be sent and summed in bfloat16 or wider, within the bound.
A program may use at most 128 MiB of HBM per device.

v0:
```python
import jax
import jax.numpy as jnp
from jax import lax
from jax.sharding import PartitionSpec as P

D = 4096
HD = 256
CONV = 4
WINDOW = 2048
BLK = 256


decay_power = 8.0
norm_epsilon = 1e-06
masked_score = -1e30


def from_behind(value, axis, steps):
    count = lax.axis_size(axis)
    leading, last = (max(0, -steps), min(count, count - steps))
    return lax.ppermute(value, axis, [(source, source + steps) for source in range(leading, last)])


def entering(value, axis, join, neutral):
    count, mine = (lax.axis_size(axis), lax.axis_index(axis))
    pieces = jax.tree.map(lambda part: lax.all_gather(part, axis), value)
    subtotal = jax.tree.map(
        lambda part, zero: jnp.full_like(part, 0) + jnp.asarray(zero, part.dtype), value, neutral
    )

    def step(position, subtotal):
        longer = join(subtotal, jax.tree.map(lambda part: part[position], pieces))
        return jax.tree.map(lambda new, old: jnp.where(position < mine, new, old), longer, subtotal)

    return lax.fori_loop(0, count - 1, step, subtotal)


def compose(earlier, later):
    return (earlier[0] * later[0], later[0] * earlier[1] + later[1])


def attend_block(query_block, window_block, query_start, key_start, head_count):
    token_rows = query_block.shape[0]
    key_count = window_block.shape[0]
    grouped = query_block.reshape(token_rows, head_count, HD)
    key_rows = window_block[:, :HD]
    value_rows = window_block[:, HD:]
    scores = jnp.einsum(
        "qhd,kd->hqk", grouped, key_rows, preferred_element_type=jnp.float32
    ) * HD ** (-0.5)
    query_pos = query_start + jnp.arange(token_rows, dtype=jnp.int32)
    key_pos = key_start + jnp.arange(key_count, dtype=jnp.int32)
    distance = query_pos[:, None] - key_pos[None, :]
    allowed = (distance >= 0) & (distance < WINDOW) & (key_pos[None, :] >= 0)
    scores = jnp.where(allowed[None], scores, masked_score)
    row_peak = jnp.max(scores, axis=2, keepdims=True)
    weights = jnp.exp(scores - row_peak)
    softmax_probs = (weights / jnp.sum(weights, axis=2, keepdims=True)).astype(jnp.bfloat16)
    output = jnp.einsum(
        "hqk,kd->qhd", softmax_probs, value_rows, preferred_element_type=jnp.float32
    )
    return output.reshape(token_rows, head_count * HD).astype(jnp.bfloat16)


def shards(
    branch_in,
    branch_gate,
    conv_taps,
    conv_shift,
    inflow_weight,
    inflow_bias,
    decay_weight,
    decay_bias,
    decay_param,
    stream,
    norm_gain,
    memory_weight,
    queries,
):
    token_rows = branch_in.shape[0]
    channels = branch_in.shape[1]
    position = lax.axis_index("seq")
    edge_rows = from_behind(branch_in[token_rows - (CONV - 1) :], "seq", 1)
    extended = jnp.concatenate([edge_rows, branch_in], axis=0).astype(jnp.float32)
    totals = conv_shift[None, :] + conv_taps[0][None, :] * extended[CONV - 1 :]
    for offset in range(1, CONV):
        totals = (
            totals
            + conv_taps[offset][None, :]
            * extended[CONV - 1 - offset : CONV - 1 - offset + token_rows]
        )
    mixed_conv = totals.astype(jnp.bfloat16)
    groups = inflow_weight.shape[0]
    grouped = mixed_conv.reshape(token_rows, groups, BLK)
    inflow = jax.nn.sigmoid(
        jnp.einsum(
            "tnb,nbc->tnc", grouped, inflow_weight, preferred_element_type=jnp.float32
        ).reshape(token_rows, channels)
        + inflow_bias[None, :]
    )
    recurrence = jax.nn.sigmoid(
        jnp.einsum(
            "tnb,nbc->tnc", grouped, decay_weight, preferred_element_type=jnp.float32
        ).reshape(token_rows, channels)
        + decay_bias[None, :]
    )
    log_decay = -decay_power * recurrence * jax.nn.softplus(-decay_param)[None, :]
    factor = jnp.exp(log_decay)
    pushed = jnp.sqrt(-jnp.expm1(2.0 * log_decay)) * inflow * mixed_conv.astype(jnp.float32)
    running_factor, running_state = lax.associative_scan(compose, (factor, pushed), axis=0)
    final_couple = (running_factor[token_rows - 1], running_state[token_rows - 1])
    start_state = jnp.zeros((channels,), jnp.float32)
    incoming = entering(
        final_couple, "seq", compose, (jnp.ones((channels,), jnp.float32), start_state)
    )[1]
    states = running_state + running_factor * incoming[None, :]
    recurrent_out = (
        states * jax.nn.gelu(branch_gate.astype(jnp.float32), approximate=True)
    ).astype(jnp.bfloat16)
    stream_float = stream.astype(jnp.float32)
    partial_squares = jnp.sum(jnp.square(stream_float), axis=1)
    scaled = (stream_float * norm_gain[None, :]).astype(jnp.bfloat16)
    partial_memory = jnp.dot(scaled, memory_weight, preferred_element_type=jnp.float32)
    summed_memory, summed_squares = lax.psum((partial_memory, partial_squares), "mp")
    memory = (summed_memory / jnp.sqrt(summed_squares / D + norm_epsilon)[:, None]).astype(
        jnp.bfloat16
    )
    shards_back = WINDOW // token_rows
    held = memory
    held_count = 1
    while held_count < shards_back + 1:
        wanted = min(held_count, shards_back + 1 - held_count)
        arrived = from_behind(held[held.shape[0] - wanted * token_rows :], "seq", held_count)
        held = jnp.concatenate([arrived, held], axis=0)
        held_count = held_count + wanted
    query_start = position * token_rows
    attended = attend_block(
        queries, held, query_start, query_start - shards_back * token_rows, queries.shape[1] // HD
    )
    return (recurrent_out, attended)


def solution(mesh):
    return jax.shard_map(
        shards,
        mesh=mesh,
        in_specs=(
            P("seq", "mp"),
            P("seq", "mp"),
            P(None, "mp"),
            P("mp"),
            P("mp", None, None),
            P("mp"),
            P("mp", None, None),
            P("mp"),
            P("mp"),
            P("seq", "mp"),
            P("mp"),
            P("mp", None),
            P("seq", "mp"),
        ),
        out_specs=(P("seq", "mp"), P("seq", "mp")),
        check_vma=False,
    )
```

profile of v0, /device:TPU:24, one launch (start us, length us, event | category | flops | bytes accessed | tf_op | source)
XLA Modules:
  0.0 259.0 jit_solution(17403985794165148722)
XLA Ops:
  8.1 3.5 %collective-permute-start = (bf16[3,1024]{1,0:T(4,128)(2,1)S(1)}, bf16[3,1024]{1,0:T(4,128)(2,1)S(1)}, u32[]{:S(2)}, u32[]{:S(2)}) collective-permute-start(bf16[3,1024]{1,0:T(4,128)(2,1)S(1)} %slice.300), channel_id=1, source_target_pairs={{0,4},{4,8},{8,12},{12,16},{16,20},{20,24},{24,28},{1,5},{5,9},{9,... | collective-permute-start | bytes 18440 | tf_op jit(solution)/shard_map/ppermute | solution.py:21
  11.6 2.9 %fusion.25 = f32[512,512]{1,0:T(8,128)} fusion(bf16[1024,512]{1,0:T(8,128)(2,1)S(1)} %copy-done, bf16[512,1024]{1,0:T(8,128)(2,1)} %param.24, f32[1024]{0:T(1024)} %param.25), kind=kOutput, calls=%fused_computation.48 | convolution fusion | flops 538443776 | bytes 3149824 | tf_op jit(solution)/shard_map/dot_general | solution.py:123
  14.9 6.3 %psum.15 = f32[512]{0:T(512)S(1)} all-reduce(f32[512]{0:T(512)S(1)} %fusion.9), channel_id=1, replica_groups=mesh['seq'=8,'mp'=4] {'mp'}, use_global_device_ids=true, to_apply=%region_4.5 | all-reduce | flops 512 | bytes 4096 | tf_op jit(solution)/shard_map/psum | solution.py:124
  21.3 3.0 %fusion.7 = pred[512,2560]{0,1:T(8,128)(4,1)} fusion(s32[2560]{0:T(1024)S(1)} %iota_add_fusion, s32[512]{0:T(512)S(1)} %iota_add_fusion.1, pred[2560]{0:T(1024)(128)(4,1)S(1)} %broadcast_compare_fusion), kind=kLoop, calls=%fused_computation.15 | loop fusion | flops 6553600 | bytes 1325568 | tf_op jit(solution)/shard_map/and | solution.py:54
  27.5 2.9 %copy.30 = f32[512,1024]{1,0:T(8,128)} copy(f32[512,1024]{0,1:T(8,128)} %bitcast.79) | data formatting | bytes 4194304 | tf_op jit(solution)/shard_map/reshape | solution.py:98
  30.5 2.9 %fusion.36 = f32[4,512,256]{1,2,0:T(8,128)} fusion(bf16[4,256,256]{2,1,0:T(8,128)(2,1)} %param.21, bf16[64,4,8,256]{3,2,1,0:T(8,128)(2,1)S(1)} %bitcast.77), kind=kOutput, calls=%fused_computation.54 | convolution fusion | flops 268435456 | bytes 3670016 | tf_op jit(solution)/shard_map/tnb,nbc->tnc/dot_general | solution.py:102
  33.4 2.9 %copy.27 = f32[512,1024]{1,0:T(8,128)} copy(f32[512,1024]{0,1:T(8,128)} %bitcast.78) | data formatting | bytes 4194304 | tf_op jit(solution)/shard_map/reshape | solution.py:104
  36.3 5.7 %convert_multiply_fusion.5 = (f32[512,1024]{1,0:T(8,128)S(1)}, f32[512,1024]{1,0:T(8,128)}) fusion(f32[512,1024]{1,0:T(8,128)} %copy.30, f32[1024]{0:T(1024)S(1)} %copy-done.18, f32[1024]{0:T(1024)S(1)} %fusion.57, f32[512,1024]{1,0:T(8,128)} %copy.27, f32[1024]{0:T(1024)S(1)} %copy-done.19, f32[515,1024]{1,0:T(8,128)S(1)} %maximum_convert_fusion, ...), kind=kLoop, calls=%fused_computation.41 | loop fusion | flops 12058624 | bytes 16809984 | tf_op jit(solution)/shard_map/mul | solution.py:109
  43.3 5.5 %slice.374 = f32[255,1024]{1,0:T(8,128)} slice(f32[512,1024]{1,0:T(8,128)} %copy-done.3), slice={[2:512:2], [0:1024:1]} | slice | bytes 2088960 | tf_op jit(solution)/shard_map/slice | solution.py:110
  48.8 5.5 %slice.312 = f32[256,1024]{1,0:T(8,128)} slice(f32[512,1024]{1,0:T(8,128)} %copy-done.3), slice={[1:512:2], [0:1024:1]} | slice | bytes 2097152 | tf_op jit(solution)/shard_map/slice | solution.py:110
  54.4 5.4 %slice.311 = f32[256,1024]{1,0:T(8,128)} slice(f32[512,1024]{1,0:T(8,128)} %copy-done.3), slice={[0:511:2], [0:1024:1]} | slice | bytes 2097152 | tf_op jit(solution)/shard_map/slice | solution.py:110
  59.8 2.8 %slice.314 = f32[256,1024]{1,0:T(8,128)} slice(f32[512,1024]{1,0:T(8,128)S(1)} %copy-done.2), slice={[0:511:2], [0:1024:1]} | slice | bytes 2097152 | tf_op jit(solution)/shard_map/slice | solution.py:110
  62.6 2.8 %slice.310 = f32[256,1024]{1,0:T(8,128)} slice(f32[512,1024]{1,0:T(8,128)S(1)} %copy-done.2), slice={[1:512:2], [0:1024:1]} | slice | bytes 2097152 | tf_op jit(solution)/shard_map/slice | solution.py:110
  65.4 2.9 %slice.309 = f32[255,1024]{1,0:T(8,128)} slice(f32[512,1024]{1,0:T(8,128)S(1)} %copy-done.2), slice={[2:512:2], [0:1024:1]} | slice | bytes 2088960 | tf_op jit(solution)/shard_map/slice | solution.py:110
  68.4 2.7 %multiply_add_fusion = (f32[256,1024]{1,0:T(8,128)S(1)}, f32[256,1024]{1,0:T(8,128)S(1)}) fusion(f32[256,1024]{1,0:T(8,128)} %slice.312, f32[256,1024]{1,0:T(8,128)} %slice.310, f32[256,1024]{1,0:T(8,128)} %slice.311, f32[256,1024]{1,0:T(8,128)} %slice.314), kind=kLoop, calls=%fused_computation.64 | loop fusion | flops 786432 | bytes 6291456 | tf_op jit(solution)/shard_map/add | solution.py:39
  83.3 2.1 pad.125
  85.4 4.6 %pad.143 = f32[256,1024]{1,0:T(8,128)} pad(f32[128,1024]{1,0:T(8,128)} %add.336, f32[]{:T(128)} %constant.25.clone.1), padding=1_0_1x0_0_0 | pad | bytes 1572868 | tf_op jit(solution)/shard_map/pad | solution.py:110
  90.0 3.5 %fusion.38 = (f32[255,1024]{1,0:T(8,128)S(1)}, f32[255,1024]{1,0:T(8,128)}) fusion(f32[255,1024]{1,0:T(8,128)} %slice.374, f32[255,1024]{1,0:T(8,128)} %slice.309, f32[256,1024]{1,0:T(8,128)S(1)} %pad.125, f32[256,1024]{1,0:T(8,128)S(1)} %pad.124, f32[256,1024]{1,0:T(8,128)} %pad.143, f32[256,1024]{1,0:T(8,128)S(1)} %pad.142), kind=kLoop, calls=%fused_computation.58 | loop fusion | flops 1305600 | bytes 8355840 | tf_op jit(solution)/shard_map/add | solution.py:39
  94.6 2.3 divide_convert_fusion.4
  99.0 2.3 pad_maximum_fusion.2
  103.6 4.3 %pad.144 = f32[512,1024]{1,0:T(8,128)S(1)} pad(f32[256,1024]{1,0:T(8,128)} %pad_maximum_fusion.2, f32[]{:T(128)} %constant.25.clone.1), padding=0_1_1x0_0_0 | pad | bytes 3145732 | tf_op jit(solution)/shard_map/pad | solution.py:110
  107.9 4.8 %pad.126 = f32[512,1024]{1,0:T(8,128)} pad(f32[256,1024]{1,0:T(8,128)S(1)} %copy-done.6, f32[]{:T(128)} %constant.25.clone.1), padding=0_1_1x0_0_0 | pad | bytes 3145732 | tf_op jit(solution)/shard_map/pad | solution.py:110
  112.7 8.6 %pad.127 = f32[512,1024]{1,0:T(8,128)} pad(f32[256,1024]{1,0:T(8,128)} %add.327, f32[]{:T(128)} %constant.25.clone.1), padding=1_0_1x0_0_0 | pad | bytes 3145732 | tf_op jit(solution)/shard_map/pad | solution.py:110
  122.1 29.7 %all-gather.1 = f32[8,1,1024]{2,1,0:T(1,128)S(1)} all-gather(f32[1,1,1024]{2,1,0:T(1,128)S(1)} %add_bitcast_fusion), channel_id=1, replica_groups=mesh['seq'=8,'mp'=4] {'seq'}, dimensions={0}, use_global_device_ids=true | all-gather | bytes 36864 | tf_op jit(solution)/shard_map/all_gather | solution.py:26
  151.8 4.9 %pad.145 = f32[512,1024]{1,0:T(8,128)} pad(f32[256,1024]{1,0:T(8,128)S(1)} %copy-done.5, f32[]{:T(128)} %constant.25.clone.1), padding=1_0_1x0_0_0 | pad | bytes 3145732 | tf_op jit(solution)/shard_map/pad | solution.py:110
  157.5 30.6 %all-gather = f32[8,1,1024]{2,1,0:T(1,128)S(1)} all-gather(f32[1,1,1024]{2,1,0:T(1,128)S(1)} %add_bitcast_fusion.1), channel_id=1, replica_groups=mesh['seq'=8,'mp'=4] {'seq'}, dimensions={0}, use_global_device_ids=true | all-gather | bytes 36864 | tf_op jit(solution)/shard_map/all_gather | solution.py:26
  188.2 2.2 pad_maximum_fusion.3
  193.4 5.0 %fusion.16 = bf16[512,1024]{1,0:T(8,128)(2,1)} fusion(bf16[512,1024]{1,0:T(8,128)(2,1)S(1)} %copy-done.12, f32[512,1024]{1,0:T(8,128)S(1)} %pad.144, f32[512,1024]{1,0:T(8,128)} %pad.145, f32[512,1024]{1,0:T(8,128)} %pad.126, f32[512,1024]{1,0:T(8,128)} %pad.127, f32[1024]{0:T(1024)S(1)} %get-tuple-element.96), kind=kLoop, calls=%fused_computation.31 | loop fusion | flops 7864320 | bytes 10489856 | tf_op jit(solution)/shard_map/convert_element_type | solution.py:119
  198.4 26.7 %collective-permute-done.1 = bf16[512,512]{1,0:T(8,128)(2,1)S(1)} collective-permute-done((bf16[512,512]{1,0:T(8,128)(2,1)}, bf16[512,512]{1,0:T(8,128)(2,1)S(1)}, u32[]{:S(2)}, u32[]{:S(2)}) %collective-permute-start.1) | collective-permute-done | bytes 524320 | tf_op jit(solution)/shard_map/ppermute | solution.py:21
  225.1 2.9 %pad_maximum_fusion = bf16[2560,512]{1,0:T(8,128)(2,1)} fusion(bf16[512,512]{1,0:T(8,128)(2,1)} %divide_convert_fusion.4, bf16[512,512]{1,0:T(8,128)(2,1)} %collective-permute-done.2, bf16[1024,512]{1,0:T(8,128)(2,1)} %collective-permute-done.3, bf16[512,512]{1,0:T(8,128)(2,1)S(1)} %collective-permute-done.1), kind=kLoop, calls=%fused_computation.22 | loop fusion | flops 10485760 | bytes 5242880 | tf_op jit(solution)/shard_map/concatenate | solution.py:134
  228.0 12.5 %fusion.62 = (f32[4,512]{1,0:T(4,128)S(1)}, f32[4,512,2560]{1,2,0:T(8,128)}) fusion(pred[512,2560]{0,1:T(8,128)(4,1)S(1)} %copy-done.10, bf16[2560,512]{1,0:T(8,128)(2,1)} %pad_maximum_fusion, bf16[64,4,8,256]{3,2,1,0:T(8,128)(2,1)S(1)} %bitcast.93), kind=kOutput, calls=%fused_computation.136 | convolution fusion | flops 2705328640 | bytes 24649728 | tf_op jit(solution)/shard_map/sub | solution.py:57
  240.5 10.3 %fusion.24 = bf16[256,4,512]{2,0,1:T(8,128)(2,1)S(1)} fusion(f32[4,512,2560]{1,2,0:T(8,128)} %get-tuple-element.176, f32[4,512]{1,0:T(4,128)S(1)} %get-tuple-element.175, bf16[2560,512]{1,0:T(8,128)(2,1)} %pad_maximum_fusion), kind=kOutput, calls=%fused_computation.44 | convolution fusion | flops 2695364608 | bytes 23339008 | tf_op jit(solution)/shard_map/hqk,kd->qhd/dot_general | solution.py:59
  (207 shorter events, 28.8 us)
Async XLA Ops:
  7.2 4.4 %copy-start = (bf16[1024,512]{1,0:T(8,128)(2,1)S(1)}, bf16[1024,512]{1,0:T(8,128)(2,1)}, u32[]{:S(2)}) copy-start(bf16[1024,512]{1,0:T(8,128)(2,1)} %param.26) | copy-start | bytes 3145732
  7.2 87.4 %all-reduce.38.cloned.1.call-start = ((), (), s32[]{:S(2)}) async-start(), calls=%async_computation | async-start | bytes 2097152 | tf_op jit(solution)/shard_map/psum | solution.py:124
  8.0 6.5 %copy-start.13 = (bf16[512,1024]{1,0:T(8,128)(2,1)S(1)}, bf16[512,1024]{1,0:T(8,128)(2,1)}, u32[]{:S(2)}) copy-start(bf16[512,1024]{1,0:T(8,128)(2,1)} %param.24) | copy-start | bytes 3145732
  8.0 13.2 %copy-start.17 = (f32[1024]{0:T(1024)S(1)}, f32[1024]{0:T(1024)}, u32[]{:S(2)}) copy-start(f32[1024]{0:T(1024)} %param.23) | copy-start | bytes 12292
  8.0 13.2 %copy-start.15 = (f32[4,1024]{1,0:T(4,128)S(1)}, f32[4,1024]{1,0:T(4,128)}, u32[]{:S(2)}) copy-start(f32[4,1024]{1,0:T(4,128)} %param.17) | copy-start | bytes 49156
  8.1 16.2 %collective-permute-start = (bf16[3,1024]{1,0:T(4,128)(2,1)S(1)}, bf16[3,1024]{1,0:T(4,128)(2,1)S(1)}, u32[]{:S(2)}, u32[]{:S(2)}) collective-permute-start(bf16[3,1024]{1,0:T(4,128)(2,1)S(1)} %slice.300), channel_id=1, source_target_pairs={{0,4},{4,8},{8,12},{12,16},{16,20},{20,24},{24,28},{1,5},{5,9},{9,... | collective-permute-start | bytes 18440 | tf_op jit(solution)/shard_map/ppermute | solution.py:21
  14.5 9.8 %copy-start.11 = (bf16[512,1024]{1,0:T(8,128)(2,1)S(1)}, bf16[512,1024]{1,0:T(8,128)(2,1)}, u32[]{:S(2)}) copy-start(bf16[512,1024]{1,0:T(8,128)(2,1)} %param.15) | copy-start | bytes 3145732
  21.3 3.4 %copy-start.16 = (f32[1024]{0:T(1024)S(1)}, f32[1024]{0:T(1024)}, u32[]{:S(2)}) copy-start(f32[1024]{0:T(1024)} %param.18) | copy-start | bytes 12292
  24.7 1.1 copy-start.14
  33.4 2.9 %copy-start.18 = (f32[1024]{0:T(1024)S(1)}, f32[1024]{0:T(1024)}, u32[]{:S(2)}) copy-start(f32[1024]{0:T(1024)} %param.20) | copy-start | bytes 12292
  33.4 2.9 %copy-start.19 = (f32[1024]{0:T(1024)S(1)}, f32[1024]{0:T(1024)}, u32[]{:S(2)}) copy-start(f32[1024]{0:T(1024)} %param.22) | copy-start | bytes 12292
  42.0 1.3 copy-start.3
  48.8 10.9 %copy-start.2 = (f32[512,1024]{1,0:T(8,128)S(1)}, f32[512,1024]{1,0:T(8,128)}, u32[]{:S(2)}) copy-start(f32[512,1024]{1,0:T(8,128)} %get-tuple-element.132) | copy-start | bytes 6291460
  79.2 1.8 copy-start.7
  79.2 1.8 copy-start.8
  82.1 1.0 copy-start.9
  94.6 6.7 %copy-start.4 = (f32[256,1024]{1,0:T(8,128)S(1)}, f32[256,1024]{1,0:T(8,128)}, u32[]{:S(2)}) copy-start(f32[256,1024]{1,0:T(8,128)} %pad.143) | copy-start | bytes 3145732
  96.9 91.3 %collective-permute-start.2 = (bf16[512,512]{1,0:T(8,128)(2,1)}, bf16[512,512]{1,0:T(8,128)(2,1)}, u32[]{:S(2)}, u32[]{:S(2)}) collective-permute-start(bf16[512,512]{1,0:T(8,128)(2,1)} %divide_convert_fusion.4), channel_id=1, source_target_pairs={{0,4},{4,8},{8,12},{12,16},{16,20},{20,24},{24,28},{1,5},{5,9},{9,... | collective-permute-start | bytes 1572872 | tf_op jit(solution)/shard_map/ppermute | solution.py:21
  103.6 4.3 %copy-start.6 = (f32[256,1024]{1,0:T(8,128)S(1)}, f32[256,1024]{1,0:T(8,128)}, u32[]{:S(2)}) copy-start(f32[256,1024]{1,0:T(8,128)} %pad_maximum_fusion.1) | copy-start | bytes 3145732
  112.7 39.1 %copy-start.5 = (f32[256,1024]{1,0:T(8,128)S(1)}, f32[256,1024]{1,0:T(8,128)}, u32[]{:S(2)}) copy-start(f32[256,1024]{1,0:T(8,128)} %add.337) | copy-start | bytes 3145732
  156.7 36.7 %copy-start.12 = (bf16[512,1024]{1,0:T(8,128)(2,1)S(1)}, bf16[512,1024]{1,0:T(8,128)(2,1)}, u32[]{:S(2)}) copy-start(bf16[512,1024]{1,0:T(8,128)(2,1)} %param.16) | copy-start | bytes 3145732
  190.4 34.7 %collective-permute-start.3 = (bf16[1024,512]{1,0:T(8,128)(2,1)}, bf16[1024,512]{1,0:T(8,128)(2,1)}, u32[]{:S(2)}, u32[]{:S(2)}) collective-permute-start(bf16[1024,512]{1,0:T(8,128)(2,1)} %pad_maximum_fusion.3), channel_id=1, source_target_pairs={{0,8},{4,12},{8,16},{12,20},{16,24},{20,28},{1,9},{5,13},{9,17},{1... | collective-permute-start | bytes 3145736 | tf_op jit(solution)/shard_map/ppermute | solution.py:21
  192.1 33.0 %collective-permute-start.1 = (bf16[512,512]{1,0:T(8,128)(2,1)}, bf16[512,512]{1,0:T(8,128)(2,1)S(1)}, u32[]{:S(2)}, u32[]{:S(2)}) collective-permute-start(bf16[512,512]{1,0:T(8,128)(2,1)} %divide_convert_fusion.4), channel_id=1, source_target_pairs={{0,16},{4,20},{8,24},{12,28},{1,17},{5,21},{9,25},{13,29},{2,18},{... | collective-permute-start | bytes 1572872 | tf_op jit(solution)/shard_map/ppermute | solution.py:21
  198.4 29.6 %copy-start.10 = (pred[512,2560]{0,1:T(8,128)(4,1)S(1)}, pred[512,2560]{0,1:T(8,128)(4,1)}, u32[]{:S(2)}) copy-start(pred[512,2560]{0,1:T(8,128)(4,1)} %fusion.7) | copy-start | bytes 3932164
  198.4 29.6 %copy-start.20 = (bf16[512,1024]{1,0:T(8,128)(2,1)S(1)}, bf16[512,1024]{1,0:T(8,128)(2,1)}, u32[]{:S(2)}) copy-start(bf16[512,1024]{1,0:T(8,128)(2,1)} %param.27) | copy-start | bytes 3145732
  240.5 11.7 %copy-start.1 = (bf16[1024,512]{1,0:T(8,128)(2,1)S(1)}, bf16[1024,512]{1,0:T(8,128)(2,1)}, u32[]{:S(2)}) copy-start(bf16[1024,512]{1,0:T(8,128)(2,1)} %param.26) | copy-start | bytes 3145732
Sparse Core Ops, SparseCore 0:
  14.7 36.3 all-reduce.37
where the time goes:
time: 260 us; the launch traced here: 259 us
  local copies, waits for them, and re-layouts  71.6 us (28%)
  blocking collectives  66.6 us (26%)
  other arithmetic  40 us (15%)
  matrix products  30.4 us (12%)
  waiting for transfers between devices  26.7 us (10%)
  between operations  15 us (6%)
  starting transfers between devices  8.24 us (3%)
    all_gather x2, blocking collectives, entering(): pieces = jax.tree.map(lambda part: lax.all_gather(part, axis), value)  60.3 us
    slice x60, local copies, waits for them, and re-layouts, shards(): lax.associative_scan(compose, (factor, pushed), axis=0)  30.9 us
    pad x32, local copies, waits for them, and re-layouts, shards(): lax.associative_scan(compose, (factor, pushed), axis=0)  30.3 us
    ppermute x4, waiting for transfers between devices, from_behind(): lax.ppermute(value, axis, [(source, source + steps) for source in range(l...  26.7 us
    sub x1, matrix products, attend_block(): weights = jnp.exp(scores - row_peak)  12.5 us
    dot_general x1, matrix products, attend_block(): jnp.einsum('hqk,kd->qhd', softmax_probs, value_rows, preferred_element_ty...  10.3 us
    ppermute x4, starting transfers between devices, from_behind(): lax.ppermute(value, axis, [(source, source + steps) for source in range(l...  8.2 us
    add x16, other arithmetic, compose(): return (earlier[0] * later[0], later[0] * earlier[1] + later[1])  7.78 us
  transfers between devices with their start and end apart: 5, of which 1 were waited for; matrix products, arithmetic and copies ran while one was open for 41% of the time, Pallas kernels for 0%

commit v1 on v0

v1 whole, which is shorter than its diff:
```python
import functools

import jax
import jax.numpy as jnp
from jax import lax
from jax.experimental import pallas as pl
from jax.experimental.pallas import tpu as pltpu
from jax.sharding import PartitionSpec as P

HD = 256
CONV = 4
WINDOW = 2048
BLK = 256
HALO = 16
CHUNK = 128
QROWS = 256
MESH = pl.DeviceIdType.MESH
F32 = jnp.float32
BF16 = jnp.bfloat16

decay_power = 8.0
norm_epsilon = 1e-06
masked_score = -1e30


def neg_expm1(x):
    series = 1.0 + x * (1.0 / 7.0)
    for k in (6.0, 5.0, 4.0, 3.0, 2.0):
        series = 1.0 + x * (1.0 / k) * series
    return jnp.where(x > -0.5, -x * series, 1.0 - jnp.exp(x))


def exchange_kernel(
    n, mp, back, far,
    taps, shift, ibias, dbias, dparam, gain,
    branch_h, gate_h, iw_h, dw_h, stream_h, mw_h,
    rec_out, kv,
    ext, gate, iw, dw, stream, mw, a_s, b_s, pairs,
    own, p_send, p_recv, ps_send, ps_recv, own_sq, y_send, y_recv, ys_send, ys_recv,
    lsem, esem, psem, ysem, csend, crecv, zs, zr, xs, xr, ds, dr,
):
    seq = lax.axis_index("seq")
    m = lax.axis_index("mp")
    core = lax.rem(m, 2)
    odd = lax.rem(seq, 2)
    mate = m + 1 - 2 * core
    T, C = rec_out.shape
    half = T // 2
    chunks = half // CHUNK
    groups = C // BLK
    peers = mp // 2
    own_base = core * half
    other_base = (1 - core) * half

    def local(src, dst, k):
        return pltpu.make_async_copy(src, dst, lsem.at[k])

    def rows(base, ch):
        return pl.ds(pl.multiple_of(base + ch * CHUNK, CHUNK), CHUNK)

    halves = [pl.ds(pl.multiple_of(b, CHUNK), half) for b in (other_base, own_base)]
    loads = [
        local(mw_h, mw, 0),
        local(stream_h.at[halves[0]], stream.at[halves[0]], 1),
        local(stream_h.at[halves[1]], stream.at[halves[1]], 2),
        local(branch_h, ext.at[pl.ds(HALO, T)], 3),
        local(iw_h, iw, 4),
        local(dw_h, dw, 5),
        local(gate_h, gate, 6),
    ]
    for load in loads:
        load.start()

    @pl.when(seq == 0)
    def _():
        ext[pl.ds(0, HALO), :] = jnp.zeros((HALO, C), BF16)

    for d in range(1, far + 1):
        @pl.when(seq < d)
        def _():
            kv[far - d] = jnp.zeros((T, kv.shape[2]), BF16)

    barrier = pltpu.get_barrier_semaphore()

    def greet(j, _):
        @pl.when(j != seq)
        def _():
            pl.semaphore_signal(barrier, inc=1, device_id=(j, m), device_id_type=MESH)
        return 0

    lax.fori_loop(0, n, greet, 0)
    for r in range(1, mp):
        pl.semaphore_signal(barrier, inc=1, device_id=(seq, lax.rem(m + r, mp)), device_id_type=MESH)
    pl.semaphore_wait(barrier, n - 1 + mp - 1)

    def remote(src, dst, ssem, rsem, to):
        return pltpu.make_async_remote_copy(
            src_ref=src, dst_ref=dst, send_sem=ssem, recv_sem=rsem, device_id=to, device_id_type=MESH
        )

    edge = remote(
        branch_h.at[pl.ds(T - HALO, HALO)], ext.at[pl.ds(0, HALO)], esem.at[0], esem.at[1], (seq + 1, m)
    )

    @pl.when(seq + 1 < n)
    def _():
        edge.start()

    def partial(base, ch):
        x = stream[rows(base, ch), :].astype(F32)
        square = jnp.sum(x * x, axis=1, keepdims=True)
        square = jnp.transpose(jnp.broadcast_to(square, (CHUNK, 128)))[:8]
        scaled = (x * gain[...]).astype(BF16)
        return jnp.dot(scaled, mw[...], preferred_element_type=F32), square

    def mate_copies(ch):
        return (
            remote(p_send.at[ch], p_recv.at[ch], psem.at[0, ch], psem.at[1, ch], (seq, mate)),
            remote(ps_send.at[ch], ps_recv.at[ch], psem.at[2, ch], psem.at[3, ch], (seq, mate)),
        )

    def peer_copies(r, ch):
        to = (seq, lax.rem(m + 2 * r, mp))
        return (
            remote(y_send.at[ch], y_recv.at[r - 1, ch], ysem.at[0, r - 1, ch], ysem.at[1, r - 1, ch], to),
            remote(ys_send.at[ch], ys_recv.at[r - 1, ch], ysem.at[2, r - 1, ch], ysem.at[3, r - 1, ch], to),
        )

    loads[0].wait()
    loads[1].wait()
    for ch in range(chunks):
        p_send[ch], ps_send[ch] = partial(other_base, ch)
        for copy in mate_copies(ch):
            copy.start()
    loads[2].wait()
    for ch in range(chunks):
        own[ch], own_sq[ch] = partial(own_base, ch)
    for ch in range(chunks):
        for copy in mate_copies(ch):
            copy.wait_recv()
        y_send[ch] = (own[ch] + p_recv[ch]).astype(BF16)
        ys_send[ch] = own_sq[ch] + ps_recv[ch]
        for r in range(1, peers):
            for copy in peer_copies(r, ch):
                copy.start()

    loads[3].wait()
    loads[4].wait()
    loads[5].wait()

    @pl.when(seq > 0)
    def _():
        edge.wait_recv()

    def gates(g, _):
        lanes = pl.ds(pl.multiple_of(g * BLK, BLK), BLK)
        soft = jnp.log1p(jnp.exp(-dparam[:, lanes]))
        row8 = lax.broadcasted_iota(jnp.int32, (1, 8, BLK), 1)

        def tile(t, _):
            x = ext[pl.ds(pl.multiple_of(t * CHUNK, CHUNK), CHUNK + HALO), lanes].astype(F32)
            total = shift[:, lanes] + taps[pl.ds(0, 1), lanes] * x[HALO:]
            for k in range(1, CONV):
                total = total + taps[pl.ds(k, 1), lanes] * pltpu.roll(x, k, 0)[HALO:]
            mixed = total.astype(BF16)
            inflow = jax.nn.sigmoid(jnp.dot(mixed, iw[g], preferred_element_type=F32) + ibias[:, lanes])
            rec = jax.nn.sigmoid(jnp.dot(mixed, dw[g], preferred_element_type=F32) + dbias[:, lanes])
            log_decay = (-decay_power * soft) * rec
            a = jnp.exp(log_decay)
            b = jnp.sqrt(neg_expm1(2.0 * log_decay)) * inflow * mixed.astype(F32)
            a = a.reshape(CHUNK // 8, 8, BLK)
            b = b.reshape(CHUNK // 8, 8, BLK)
            for k in (1, 2, 4):
                keep = row8 >= k
                b = b + a * jnp.where(keep, pltpu.roll(b, k, 1), 0.0)
                a = a * jnp.where(keep, pltpu.roll(a, k, 1), 1.0)
            here = pl.ds(pl.multiple_of(t * CHUNK, CHUNK), CHUNK)
            a_s[here, lanes] = a.reshape(CHUNK, BLK)
            b_s[here, lanes] = b.reshape(CHUNK, BLK)
            return 0

        lax.fori_loop(0, T // CHUNK, tile, 0)
        return 0

    lax.fori_loop(0, groups // 2, gates, 0)

    def z_copy(d, ch):
        at = rows(own_base, ch)
        return remote(kv.at[far - d, at], kv.at[far - d - 2, at], zs.at[d, ch], zr.at[d + 2, ch], (seq + 2, m))

    def z_arrival(d, ch):
        at = rows(own_base, ch)
        return remote(kv.at[far - d, at], kv.at[far - d, at], zs.at[d, ch], zr.at[d, ch], (seq, mate))

    def x_copy(d, e, ch):
        at = rows(own_base, ch)
        return remote(
            kv.at[far - d, at], kv.at[far - e, at], xs.at[d, ch], xr.at[e, ch], (seq + (e - d), m)
        )

    def x_arrival(d, ch):
        at = rows(own_base, ch)
        return remote(kv.at[far - d, at], kv.at[far - d, at], xs.at[d, ch], xr.at[d, ch], (seq, mate))

    def d_copy(d, ch):
        at = rows(own_base, ch)
        return remote(kv.at[far - d, at], kv.at[far - d, at], ds.at[d, ch], dr.at[d, ch], (seq, mate))

    def d_arrival(d, ch):
        at = rows(other_base, ch)
        return remote(kv.at[far - d, at], kv.at[far - d, at], ds.at[d, ch], dr.at[d, ch], (seq, mate))

    def even_copies(d, ch, act):
        if d + 2 <= far:
            @pl.when((seq >= d) & (seq + 2 < n))
            def _():
                act(z_copy(d, ch))
        if d >= 2:
            @pl.when((seq >= d) & (odd == 1))
            def _():
                act(x_copy(d, d - 1, ch))
        if d + 1 <= back:
            @pl.when((seq >= d) & (odd == 0))
            def _():
                act(x_copy(d, d + 1, ch))

    def mate_out(d, ch, act):
        if d <= back:
            @pl.when(seq >= d)
            def _():
                act(d_copy(d, ch))

    start = lambda copy: copy.start()
    features = C * mp
    for ch in range(chunks):
        for r in range(1, peers):
            for copy in peer_copies(r, ch):
                copy.wait_recv()
        total = y_send[ch].astype(F32)
        square = ys_send[ch]
        for r in range(1, peers):
            total = total + y_recv[r - 1, ch].astype(F32)
            square = square + ys_recv[r - 1, ch]
        inverse = 1.0 / jnp.sqrt(square / features + norm_epsilon)
        inverse = jnp.transpose(jnp.broadcast_to(inverse[:1], (128, CHUNK)))
        kv[far, rows(own_base, ch), :] = (total * inverse[:, :1]).astype(BF16)
        even_copies(0, ch, start)
        mate_out(0, ch, start)

    lax.fori_loop(groups // 2, groups, gates, 0)

    def carry_rows(j, state):
        factor, value = state
        at = pl.ds(pl.multiple_of(j * 8, 8), 8)
        a = a_s[at, :]
        b = b_s[at, :] + a * value
        a = a * factor
        a_s[at, :] = a
        b_s[at, :] = b
        return jnp.broadcast_to(a[7:8], (8, C)), jnp.broadcast_to(b[7:8], (8, C))

    factor, value = lax.fori_loop(0, T // 8, carry_rows, (jnp.ones((8, C), F32), jnp.zeros((8, C), F32)))
    pairs[seq, pl.ds(0, 1), :] = factor[:1]
    pairs[seq, pl.ds(1, 1), :] = value[:1]

    def pair_copy(j):
        return remote(pairs.at[seq], pairs.at[seq], csend.at[j], crecv.at[seq], (j, m))

    def pair_arrival(j):
        return remote(pairs.at[j], pairs.at[j], csend.at[j], crecv.at[j], (seq, mate))

    def send_pair(j, _):
        pair_copy(j).start()
        return 0

    lax.fori_loop(seq + 1, n, send_pair, 0)

    def forward(d):
        for ch in range(chunks):
            @pl.when(seq >= d)
            def _():
                z_arrival(d, ch).wait_recv()
            even_copies(d, ch, start)
            mate_out(d, ch, start)

    if far >= 2:
        forward(2)

    loads[6].wait()

    def join(j, incoming):
        pair_arrival(j).wait_recv()
        return pairs[j, pl.ds(0, 1), :] * incoming + pairs[j, pl.ds(1, 1), :]

    incoming = lax.fori_loop(0, seq, join, jnp.zeros((1, C), F32))

    def finish(j, _):
        at = pl.ds(pl.multiple_of(j * 16, 16), 16)
        states = b_s[at, :] + a_s[at, :] * incoming
        v = gate[at, :].astype(F32)
        gelu = 0.5 * v * (1.0 + jnp.tanh(0.7978845608028654 * (v + 0.044715 * v * v * v)))
        rec_out[at, :] = (states * gelu).astype(BF16)
        return 0

    lax.fori_loop(0, T // 16, finish, 0)

    for d in range(4, far + 1, 2):
        forward(d)
    for d in range(1, back + 1, 2):
        for ch in range(chunks):
            @pl.when(seq >= d)
            def _():
                x_arrival(d, ch).wait_recv()
            mate_out(d, ch, start)

    for d in range(back + 1):
        for ch in range(chunks):
            @pl.when(seq >= d)
            def _():
                d_arrival(d, ch).wait_recv()
    sent = lambda copy: copy.wait_send()
    for ch in range(chunks):
        for copy in mate_copies(ch):
            copy.wait_send()
        for r in range(1, peers):
            for copy in peer_copies(r, ch):
                copy.wait_send()
        for d in range(0, far + 1, 2):
            even_copies(d, ch, sent)
        for d in range(back + 1):
            mate_out(d, ch, sent)

    @pl.when(seq + 1 < n)
    def _():
        edge.wait_send()

    def pair_sent(j, _):
        pair_copy(j).wait_send()
        return 0

    lax.fori_loop(seq + 1, n, pair_sent, 0)


def attend_kernel(back, T, q_ref, kv_ref, out_ref, s_ref):
    seq = lax.axis_index("seq")
    first = pl.program_id(1) * QROWS
    steps = WINDOW // QROWS + 1
    q = q_ref[...]
    scale = HD ** (-0.5)
    row = lax.broadcasted_iota(jnp.int32, (QROWS, QROWS), 0)
    col = lax.broadcasted_iota(jnp.int32, (QROWS, QROWS), 1)
    peak = jnp.full((QROWS, QROWS), masked_score, F32)
    for k in range(steps):
        at = first + k * QROWS
        keys = kv_ref[pl.ds(pl.multiple_of(at, QROWS), QROWS), pl.ds(0, HD)]
        s = lax.dot_general(q, keys, (((1,), (1,)), ((), ())), preferred_element_type=F32) * scale
        if k == 0:
            s = jnp.where(col > row, s, masked_score)
        if k == steps - 1:
            s = jnp.where(col <= row, s, masked_score)
        else:
            s = jnp.where(at >= (back - seq) * T, s, masked_score)
        s_ref[:, pl.ds(k * QROWS, QROWS)] = s
        peak = jnp.maximum(peak, s)
    peak = jnp.max(peak, axis=1, keepdims=True)
    total = jnp.zeros((QROWS, QROWS), F32)
    acc = jnp.zeros((QROWS, HD), F32)
    for k in range(steps):
        p = jnp.exp(s_ref[:, pl.ds(k * QROWS, QROWS)] - peak)
        total = total + p
        values = kv_ref[pl.ds(pl.multiple_of(first + k * QROWS, QROWS), QROWS), pl.ds(HD, HD)]
        acc = acc + jnp.dot(p.astype(BF16), values, preferred_element_type=F32)
    out_ref[...] = (acc / jnp.sum(total, axis=1, keepdims=True)).astype(BF16)


def shards(
    n, mp,
    branch_in, branch_gate, conv_taps, conv_shift, inflow_weight, inflow_bias, decay_weight, decay_bias,
    decay_param, stream, norm_gain, memory_weight, queries,
):
    T, C = branch_in.shape
    width = memory_weight.shape[1]
    back = WINDOW // T
    far = back + back % 2
    chunks = T // 2 // CHUNK
    groups = inflow_weight.shape[0]
    peers = mp // 2
    vmem = pl.BlockSpec(memory_space=pltpu.VMEM)
    hbm = pl.BlockSpec(memory_space=pl.ANY)
    dma = pltpu.SemaphoreType.DMA
    flat = lambda v: v.reshape(1, -1)
    others = max(peers - 1, 1)
    recurrent_out, kv = pl.pallas_call(
        functools.partial(exchange_kernel, n, mp, back, far),
        out_shape=(
            jax.ShapeDtypeStruct((T, C), BF16),
            jax.ShapeDtypeStruct((far + 1, T, width), BF16),
        ),
        in_specs=[vmem] * 6 + [hbm] * 6,
        out_specs=(vmem, vmem),
        scratch_shapes=[
            pltpu.VMEM((T + HALO, C), BF16),
            pltpu.VMEM((T, C), BF16),
            pltpu.VMEM((groups, BLK, BLK), BF16),
            pltpu.VMEM((groups, BLK, BLK), BF16),
            pltpu.VMEM((T, C), BF16),
            pltpu.VMEM((C, width), BF16),
            pltpu.VMEM((T, C), F32),
            pltpu.VMEM((T, C), F32),
            pltpu.VMEM((n, 2, C), F32),
            pltpu.VMEM((chunks, CHUNK, width), F32),
            pltpu.VMEM((chunks, CHUNK, width), F32),
            pltpu.VMEM((chunks, CHUNK, width), F32),
            pltpu.VMEM((chunks, 8, CHUNK), F32),
            pltpu.VMEM((chunks, 8, CHUNK), F32),
            pltpu.VMEM((chunks, 8, CHUNK), F32),
            pltpu.VMEM((chunks, CHUNK, width), BF16),
            pltpu.VMEM((others, chunks, CHUNK, width), BF16),
            pltpu.VMEM((chunks, 8, CHUNK), F32),
            pltpu.VMEM((others, chunks, 8, CHUNK), F32),
            dma((7,)),
            dma((2,)),
            dma((4, chunks)),
            dma((4, others, chunks)),
            dma((n,)),
            dma((n,)),
        ]
        + [dma((far + 3, chunks))] * 6,
        compiler_params=pltpu.CompilerParams(collective_id=0, has_side_effects=True),
    )(
        conv_taps, flat(conv_shift), flat(inflow_bias), flat(decay_bias), flat(decay_param), flat(norm_gain),
        branch_in, branch_gate, inflow_weight, decay_weight, stream, memory_weight,
    )
    window = kv[far - back:].reshape((back + 1) * T, width)
    heads = queries.shape[1] // HD
    attended = pl.pallas_call(
        functools.partial(attend_kernel, back, T),
        out_shape=jax.ShapeDtypeStruct(queries.shape, BF16),
        grid=(heads, T // QROWS),
        in_specs=[
            pl.BlockSpec((QROWS, HD), lambda h, i: (i, h)),
            pl.BlockSpec(window.shape, lambda h, i: (0, 0)),
        ],
        out_specs=pl.BlockSpec((QROWS, HD), lambda h, i: (i, h)),
        scratch_shapes=[pltpu.VMEM((QROWS, WINDOW + QROWS), F32)],
    )(queries, window)
    return recurrent_out, attended


def solution(mesh):
    return jax.shard_map(
        functools.partial(shards, mesh.shape["seq"], mesh.shape["mp"]),
        mesh=mesh,
        in_specs=(
            P("seq", "mp"),
            P("seq", "mp"),
            P(None, "mp"),
            P("mp"),
            P("mp", None, None),
            P("mp"),
            P("mp", None, None),
            P("mp"),
            P("mp"),
            P("seq", "mp"),
            P("mp"),
            P("mp", None),
            P("seq", "mp"),
        ),
        out_specs=(P("seq", "mp"), P("seq", "mp")),
        check_vma=False,
    )
```

time: 260 us -> 55.6 us (0.21)
  the two profiles are of different devices: /device:TPU:24 before, /device:TPU:17 now
where the time goes in v1:
time: 55.6 us; the launch traced here: 55.4 us
  Pallas kernels  53.7 us (97%)
  local copies, waits for them, and re-layouts  0.97 us (2%)
  between operations  0.65 us (1%)
    pallas_call x1, Pallas kernels, shards(): pl.pallas_call(functools.partial(exchange_kernel, n, mp, back, far), out_...  36.2 us
    pallas_call x1, Pallas kernels, shards(): pl.pallas_call(functools.partial(attend_kernel, back, T), out_shape=jax.S...  17.5 us

profile of v1, /device:TPU:17, one launch (start us, length us, event | category | flops | bytes accessed | tf_op | source)
XLA Modules:
  0.0 55.4 jit_solution(14878082128426247621)
XLA Ops:
  0.6 36.2 %shard_map.140 = (bf16[512,1024]{1,0:T(8,128)(2,1)}, bf16[5,512,512]{2,1,0:T(8,128)(2,1)}) custom-call(f32[4,1024]{1,0:T(4,128)} %taps.1, f32[1,1024]{1,0:T(1,128)} %bitcast.7, f32[1,1024]{1,0:T(1,128)} %bitcast.8, f32[1,1024]{1,0:T(1,128)} %bitcast.9, f32[1,1024]{1,0:T(1,128)} %bitcast.10, f32[1,1024]{1,0:T(1,128)} %bitcast.11, bf16[512,1024]{1,0:T(8,128)(2,1)} %branch_h.1, ...), custom_call_target="tpu_custom_call" | custom-call | tf_op jit(solution)/shard_map/pallas_call | solution.py:393
  36.9 0.0 copy-start
  36.9 17.5 %shard_map.141 = bf16[512,1024]{1,0:T(8,128)(2,1)} custom-call(bf16[512,1024]{1,0:T(8,128)(2,1)} %q_ref.1, bf16[2560,512]{1,0:T(8,128)(2,1)} %bitcast.6), custom_call_target="tpu_custom_call" | custom-call | tf_op jit(solution)/shard_map/pallas_call | solution.py:436
  54.4 0.0 copy-done
  54.4 1.0 %copy.16 = bf16[512,1024]{1,0:T(8,128)(2,1)} copy(bf16[512,1024]{1,0:T(8,128)(2,1)S(1)} %copy-done) | data formatting | bytes 2097152
Async XLA Ops:
  36.9 17.5 %copy-start = (bf16[512,1024]{1,0:T(8,128)(2,1)S(1)}, bf16[512,1024]{1,0:T(8,128)(2,1)}, u32[]{:S(2)}) copy-start(bf16[512,1024]{1,0:T(8,128)(2,1)} %get-tuple-element.8) | copy-start | bytes 3145732

commit v2 on v1

--- a/solution.py
+++ b/solution.py
@@ -33,8 +33,9 @@
 def exchange_kernel(
     n, mp, back, far,
     taps, shift, ibias, dbias, dparam, gain,
-    branch_h, gate_h, iw_h, dw_h, stream_h, mw_h,
-    rec_out, kv,
+    branch_h, gate_h, iw_h, dw_h, stream_h, mw_h, q_h,
+    rec_out, att_out,
+    kv, q_v, acc_s, peak_s, sum_s,
     ext, gate, iw, dw, stream, mw, a_s, b_s, pairs,
     own, p_send, p_recv, ps_send, ps_recv, own_sq, y_send, y_recv, ys_send, ys_recv,
     lsem, esem, psem, ysem, csend, crecv, zs, zr, xs, xr, ds, dr,
@@ -67,6 +68,7 @@
         local(iw_h, iw, 4),
         local(dw_h, dw, 5),
         local(gate_h, gate, 6),
+        local(q_h, q_v, 7),
     ]
     for load in loads:
         load.start()
@@ -74,11 +76,6 @@
     @pl.when(seq == 0)
     def _():
         ext[pl.ds(0, HALO), :] = jnp.zeros((HALO, C), BF16)
-
-    for d in range(1, far + 1):
-        @pl.when(seq < d)
-        def _():
-            kv[far - d] = jnp.zeros((T, kv.shape[2]), BF16)
 
     barrier = pltpu.get_barrier_semaphore()
 
@@ -283,41 +280,116 @@
             even_copies(d, ch, start)
             mate_out(d, ch, start)
 
+    loads[7].wait()
+
+    def scale_rows(j, _):
+        at = pl.ds(pl.multiple_of(j * 64, 64), 64)
+        q_v[at, :] = (q_v[at, :].astype(F32) * HD ** (-0.5)).astype(BF16)
+        return 0
+
+    lax.fori_loop(0, T // 64, scale_rows, 0)
     if far >= 2:
         forward(2)
 
-    loads[6].wait()
-
-    def join(j, incoming):
-        pair_arrival(j).wait_recv()
-        return pairs[j, pl.ds(0, 1), :] * incoming + pairs[j, pl.ds(1, 1), :]
-
-    incoming = lax.fori_loop(0, seq, join, jnp.zeros((1, C), F32))
-
-    def finish(j, _):
-        at = pl.ds(pl.multiple_of(j * 16, 16), 16)
-        states = b_s[at, :] + a_s[at, :] * incoming
-        v = gate[at, :].astype(F32)
-        gelu = 0.5 * v * (1.0 + jnp.tanh(0.7978845608028654 * (v + 0.044715 * v * v * v)))
-        rec_out[at, :] = (states * gelu).astype(BF16)
-        return 0
-
-    lax.fori_loop(0, T // 16, finish, 0)
-
-    for d in range(4, far + 1, 2):
-        forward(d)
-    for d in range(1, back + 1, 2):
+    row = lax.broadcasted_iota(jnp.int32, (QROWS, QROWS), 0)
+    col = lax.broadcasted_iota(jnp.int32, (QROWS, QROWS), 1)
+    tiles = T // QROWS
+    heads = q_v.shape[1] // HD
+
+    def attend_tile(d, h, i):
+        unit = h * tiles + i
+        low, high = 0, T
+        if d == 0:
+            high = (i + 1) * QROWS
+        if d == back:
+            low = i * QROWS
+        q = q_v[pl.ds(i * QROWS, QROWS), pl.ds(pl.multiple_of(h * HD, HD), HD)]
+        keys = kv[far - d, pl.ds(low, high - low), pl.ds(0, HD)]
+        values = kv[far - d, pl.ds(low, high - low), pl.ds(HD, HD)]
+        s = lax.dot_general(q, keys, (((1,), (1,)), ((), ())), preferred_element_type=F32)
+        parts = [s[:, k : k + QROWS] for k in range(0, high - low, QROWS)]
+        if d == 0:
+            parts[-1] = jnp.where(col <= row, parts[-1], masked_score)
+        if d == back:
+            parts[0] = jnp.where(col > row, parts[0], masked_score)
+        peak = functools.reduce(jnp.maximum, parts)
+        peak = jnp.max(peak, axis=1, keepdims=True)
+        if d > 0:
+            before = peak_s[unit][:, :1]
+            peak = jnp.maximum(before, peak)
+            alpha = jnp.exp(before - peak)
+        parts = [jnp.exp(part - peak) for part in parts]
+        summed = sum(part[:, k : k + 128] for part in parts for k in range(0, QROWS, 128))
+        p = jnp.concatenate([part.astype(BF16) for part in parts], axis=1)
+        gathered = jnp.dot(p, values, preferred_element_type=F32)
+        if d > 0:
+            summed = summed + alpha * sum_s[unit]
+            gathered = gathered + alpha * acc_s[unit]
+        peak_s[unit] = jnp.broadcast_to(peak, (QROWS, 128))
+        sum_s[unit] = summed
+        acc_s[unit] = gathered
+
+    def attend(d):
+        if d > back:
+            return
+
+        @pl.when(seq >= d)
+        def _():
+            for ch in range(chunks):
+                d_arrival(d, ch).wait_recv()
+
+            def head(h, _):
+                for i in range(tiles):
+                    attend_tile(d, h, i)
+                return 0
+
+            lax.fori_loop(0, heads, head, 0)
+
+    def crossed(d):
         for ch in range(chunks):
             @pl.when(seq >= d)
             def _():
                 x_arrival(d, ch).wait_recv()
             mate_out(d, ch, start)
 
-    for d in range(back + 1):
-        for ch in range(chunks):
-            @pl.when(seq >= d)
-            def _():
-                d_arrival(d, ch).wait_recv()
+    def join(j, incoming):
+        pair_arrival(j).wait_recv()
+        return pairs[j, pl.ds(0, 1), :] * incoming + pairs[j, pl.ds(1, 1), :]
+
+    def finish_recurrence():
+        incoming = lax.fori_loop(0, seq, join, jnp.zeros((1, C), F32))
+
+        def finish(j, _):
+            at = pl.ds(pl.multiple_of(j * 16, 16), 16)
+            states = b_s[at, :] + a_s[at, :] * incoming
+            v = gate[at, :].astype(F32)
+            gelu = 0.5 * v * (1.0 + jnp.tanh(0.7978845608028654 * (v + 0.044715 * v * v * v)))
+            rec_out[at, :] = (states * gelu).astype(BF16)
+            return 0
+
+        lax.fori_loop(0, T // 16, finish, 0)
+
+    attend(0)
+    for d in range(2, far + 1, 2):
+        crossed(d - 1)
+        if d == 2:
+            loads[6].wait()
+            finish_recurrence()
+        attend(d)
+        if d + 2 <= far:
+            forward(d + 2)
+        attend(d - 1)
+
+    def settle(h, _):
+        for i in range(tiles):
+            unit = h * tiles + i
+            scale = 1.0 / jnp.sum(sum_s[unit], axis=1, keepdims=True)
+            at = (pl.ds(i * QROWS, QROWS), pl.ds(pl.multiple_of(h * HD, HD), HD))
+            att_out[at] = (acc_s[unit] * scale).astype(BF16)
+        return 0
+
+    lax.fori_loop(0, heads, settle, 0)
+
     sent = lambda copy: copy.wait_send()
     for ch in range(chunks):
         for copy in mate_copies(ch):
@@ -339,38 +411,6 @@
         return 0
 
     lax.fori_loop(seq + 1, n, pair_sent, 0)
-
-
-def attend_kernel(back, T, q_ref, kv_ref, out_ref, s_ref):
-    seq = lax.axis_index("seq")
-    first = pl.program_id(1) * QROWS
-    steps = WINDOW // QROWS + 1
-    q = q_ref[...]
-    scale = HD ** (-0.5)
-    row = lax.broadcasted_iota(jnp.int32, (QROWS, QROWS), 0)
-    col = lax.broadcasted_iota(jnp.int32, (QROWS, QROWS), 1)
-    peak = jnp.full((QROWS, QROWS), masked_score, F32)
-    for k in range(steps):
-        at = first + k * QROWS
-        keys = kv_ref[pl.ds(pl.multiple_of(at, QROWS), QROWS), pl.ds(0, HD)]
-        s = lax.dot_general(q, keys, (((1,), (1,)), ((), ())), preferred_element_type=F32) * scale
-        if k == 0:
-            s = jnp.where(col > row, s, masked_score)
-        if k == steps - 1:
-            s = jnp.where(col <= row, s, masked_score)
-        else:
-            s = jnp.where(at >= (back - seq) * T, s, masked_score)
-        s_ref[:, pl.ds(k * QROWS, QROWS)] = s
-        peak = jnp.maximum(peak, s)
-    peak = jnp.max(peak, axis=1, keepdims=True)
-    total = jnp.zeros((QROWS, QROWS), F32)
-    acc = jnp.zeros((QROWS, HD), F32)
-    for k in range(steps):
-        p = jnp.exp(s_ref[:, pl.ds(k * QROWS, QROWS)] - peak)
-        total = total + p
-        values = kv_ref[pl.ds(pl.multiple_of(first + k * QROWS, QROWS), QROWS), pl.ds(HD, HD)]
-        acc = acc + jnp.dot(p.astype(BF16), values, preferred_element_type=F32)
-    out_ref[...] = (acc / jnp.sum(total, axis=1, keepdims=True)).astype(BF16)
 
 
 def shards(
@@ -390,15 +430,22 @@
     dma = pltpu.SemaphoreType.DMA
     flat = lambda v: v.reshape(1, -1)
     others = max(peers - 1, 1)
-    recurrent_out, kv = pl.pallas_call(
+    heads = queries.shape[1] // HD
+    units = heads * (T // QROWS)
+    return pl.pallas_call(
         functools.partial(exchange_kernel, n, mp, back, far),
         out_shape=(
             jax.ShapeDtypeStruct((T, C), BF16),
-            jax.ShapeDtypeStruct((far + 1, T, width), BF16),
+            jax.ShapeDtypeStruct(queries.shape, BF16),
         ),
-        in_specs=[vmem] * 6 + [hbm] * 6,
+        in_specs=[vmem] * 6 + [hbm] * 7,
         out_specs=(vmem, vmem),
         scratch_shapes=[
+            pltpu.VMEM((far + 1, T, width), BF16),
+            pltpu.VMEM(queries.shape, BF16),
+            pltpu.VMEM((units, QROWS, HD), F32),
+            pltpu.VMEM((units, QROWS, 128), F32),
+            pltpu.VMEM((units, QROWS, 128), F32),
             pltpu.VMEM((T + HALO, C), BF16),
             pltpu.VMEM((T, C), BF16),
             pltpu.VMEM((groups, BLK, BLK), BF16),
@@ -418,7 +465,7 @@
             pltpu.VMEM((others, chunks, CHUNK, width), BF16),
             pltpu.VMEM((chunks, 8, CHUNK), F32),
             pltpu.VMEM((others, chunks, 8, CHUNK), F32),
-            dma((7,)),
+            dma((8,)),
             dma((2,)),
             dma((4, chunks)),
             dma((4, others, chunks)),
@@ -429,22 +476,8 @@
         compiler_params=pltpu.CompilerParams(collective_id=0, has_side_effects=True),
     )(
         conv_taps, flat(conv_shift), flat(inflow_bias), flat(decay_bias), flat(decay_param), flat(norm_gain),
-        branch_in, branch_gate, inflow_weight, decay_weight, stream, memory_weight,
+        branch_in, branch_gate, inflow_weight, decay_weight, stream, memory_weight, queries,
     )
-    window = kv[far - back:].reshape((back + 1) * T, width)
-    heads = queries.shape[1] // HD
-    attended = pl.pallas_call(
-        functools.partial(attend_kernel, back, T),
-        out_shape=jax.ShapeDtypeStruct(queries.shape, BF16),
-        grid=(heads, T // QROWS),
-        in_specs=[
-            pl.BlockSpec((QROWS, HD), lambda h, i: (i, h)),
-            pl.BlockSpec(window.shape, lambda h, i: (0, 0)),
-        ],
-        out_specs=pl.BlockSpec((QROWS, HD), lambda h, i: (i, h)),
-        scratch_shapes=[pltpu.VMEM((QROWS, WINDOW + QROWS), F32)],
-    )(queries, window)
-    return recurrent_out, attended
 
 
 def solution(mesh):

time: 55.6 us -> 49.9 us (0.90)
  the two profiles are of different devices: /device:TPU:17 before, /device:TPU:24 now
where the time goes in v2:
time: 49.9 us; the launch traced here: 49.7 us
  Pallas kernels  45.7 us (92%)
  local copies, waits for them, and re-layouts  3.32 us (7%)
  between operations  0.65 us (1%)
    pallas_call x1, Pallas kernels, shards(): pl.pallas_call(functools.partial(exchange_kernel, n, mp, back, far), out_...  45.7 us
    unnamed x4, local copies, waits for them, and re-layouts  3.32 us

profile of v2, /device:TPU:24, one launch (start us, length us, event | category | flops | bytes accessed | tf_op | source)
XLA Modules:
  0.0 49.7 jit_solution(5649831799618417170)
XLA Ops:
  0.6 45.7 %shard_map.140 = (bf16[512,1024]{1,0:T(8,128)(2,1)}, bf16[512,1024]{1,0:T(8,128)(2,1)}) custom-call(f32[4,1024]{1,0:T(4,128)} %taps.1, f32[1,1024]{1,0:T(1,128)} %bitcast.5, f32[1,1024]{1,0:T(1,128)} %bitcast.6, f32[1,1024]{1,0:T(1,128)} %bitcast.7, f32[1,1024]{1,0:T(1,128)} %bitcast.8, f32[1,1024]{1,0:T(1,128)} %bitcast.9, bf16[512,1024]{1,0:T(8,128)(2,1)} %branch_h.1, ...), custom_call_target="tpu_custom_call" | custom-call | tf_op jit(solution)/shard_map/pallas_call | solution.py:435
  46.4 0.0 copy-start
  46.4 2.4 %copy.17 = bf16[512,1024]{1,0:T(8,128)(2,1)} copy(bf16[512,1024]{1,0:T(8,128)(2,1)} %get-tuple-element.4) | data formatting | bytes 2097152
  48.7 0.0 copy-done
  48.7 1.0 %copy.18 = bf16[512,1024]{1,0:T(8,128)(2,1)} copy(bf16[512,1024]{1,0:T(8,128)(2,1)S(1)} %copy-done) | data formatting | bytes 2097152
Async XLA Ops:
  46.4 2.4 %copy-start = (bf16[512,1024]{1,0:T(8,128)(2,1)S(1)}, bf16[512,1024]{1,0:T(8,128)(2,1)}, u32[]{:S(2)}) copy-start(bf16[512,1024]{1,0:T(8,128)(2,1)} %get-tuple-element.5) | copy-start | bytes 3145732

commit v3 on v2

--- a/solution.py
+++ b/solution.py
@@ -246,6 +246,17 @@
 
     lax.fori_loop(groups // 2, groups, gates, 0)
 
+    def forward(d):
+        for ch in range(chunks):
+            @pl.when(seq >= d)
+            def _():
+                z_arrival(d, ch).wait_recv()
+            even_copies(d, ch, start)
+            mate_out(d, ch, start)
+
+    if far >= 2:
+        forward(2)
+
     def carry_rows(j, state):
         factor, value = state
         at = pl.ds(pl.multiple_of(j * 8, 8), 8)
@@ -256,7 +267,7 @@
         b_s[at, :] = b
         return jnp.broadcast_to(a[7:8], (8, C)), jnp.broadcast_to(b[7:8], (8, C))
 
-    factor, value = lax.fori_loop(0, T // 8, carry_rows, (jnp.ones((8, C), F32), jnp.zeros((8, C), F32)))
+    factor, value = lax.fori_loop(0, T // 8, carry_rows, (jnp.ones((8, C), F32), jnp.zeros((8, C), F32)), unroll=4)
     pairs[seq, pl.ds(0, 1), :] = factor[:1]
     pairs[seq, pl.ds(1, 1), :] = value[:1]
 
@@ -271,14 +282,6 @@
         return 0
 
     lax.fori_loop(seq + 1, n, send_pair, 0)
-
-    def forward(d):
-        for ch in range(chunks):
-            @pl.when(seq >= d)
-            def _():
-                z_arrival(d, ch).wait_recv()
-            even_copies(d, ch, start)
-            mate_out(d, ch, start)
 
     loads[7].wait()
 
@@ -288,9 +291,6 @@
         return 0
 
     lax.fori_loop(0, T // 64, scale_rows, 0)
-    if far >= 2:
-        forward(2)
-
     row = lax.broadcasted_iota(jnp.int32, (QROWS, QROWS), 0)
     col = lax.broadcasted_iota(jnp.int32, (QROWS, QROWS), 1)
     tiles = T // QROWS

time: 49.9 us -> 53.7 us (1.076)
  Pallas kernels: 45.7 us -> 49.6 us
    pallas_call x1, Pallas kernels: 45.7 us -> 49.6 us  [shards(): pl.pallas_call(functools.partial(exchange_kernel, n, mp, back, far), out_...]
where the time goes in v3:
time: 53.7 us; the launch traced here: 53.5 us
  Pallas kernels  49.6 us (92%)
  local copies, waits for them, and re-layouts  3.32 us (6%)
  between operations  0.65 us (1%)
    pallas_call x1, Pallas kernels, shards(): pl.pallas_call(functools.partial(exchange_kernel, n, mp, back, far), out_...  49.6 us
    unnamed x4, local copies, waits for them, and re-layouts  3.32 us

profile of v3, /device:TPU:24, one launch (start us, length us, event | category | flops | bytes accessed | tf_op | source)
XLA Modules:
  0.0 53.5 jit_solution(2489188859013486945)
XLA Ops:
  0.6 49.6 %shard_map.140 = (bf16[512,1024]{1,0:T(8,128)(2,1)}, bf16[512,1024]{1,0:T(8,128)(2,1)}) custom-call(f32[4,1024]{1,0:T(4,128)} %taps.1, f32[1,1024]{1,0:T(1,128)} %bitcast.5, f32[1,1024]{1,0:T(1,128)} %bitcast.6, f32[1,1024]{1,0:T(1,128)} %bitcast.7, f32[1,1024]{1,0:T(1,128)} %bitcast.8, f32[1,1024]{1,0:T(1,128)} %bitcast.9, bf16[512,1024]{1,0:T(8,128)(2,1)} %branch_h.1, ...), custom_call_target="tpu_custom_call" | custom-call | tf_op jit(solution)/shard_map/pallas_call | solution.py:435
  50.2 0.0 copy-start
  50.2 2.4 %copy.17 = bf16[512,1024]{1,0:T(8,128)(2,1)} copy(bf16[512,1024]{1,0:T(8,128)(2,1)} %get-tuple-element.4) | data formatting | bytes 2097152
  52.6 0.0 copy-done
  52.6 1.0 %copy.18 = bf16[512,1024]{1,0:T(8,128)(2,1)} copy(bf16[512,1024]{1,0:T(8,128)(2,1)S(1)} %copy-done) | data formatting | bytes 2097152
Async XLA Ops:
  50.2 2.4 %copy-start = (bf16[512,1024]{1,0:T(8,128)(2,1)S(1)}, bf16[512,1024]{1,0:T(8,128)(2,1)}, u32[]{:S(2)}) copy-start(bf16[512,1024]{1,0:T(8,128)(2,1)} %get-tuple-element.5) | copy-start | bytes 3145732
